TPU v7x, 512 devices: a whole 4x8x8 slice. The times are simulated.
512 devices in a mesh: row: 16 (over y, core), col: 32 (over z, x).
Axes of the slice: x: 4, y: 8, z: 8, core: 2. Of those that a mesh axis runs over, the one named last changes fastest.
Arguments:
- offsets: float32 [3, 131072], P(None, ('row', 'col')), may hold values from 0 to 11
- cells: int32 [3, 1024], replicated, may hold values from 0 to 15, as said below
- types: int32 [131072], P(('row', 'col')), may hold values from 0 to 3, as said below
- mask: int32 [16, 64, 16, 64], P(None, 'col', 'row'), may hold values from 0 to 1, as said below
- chi_table: float32 [4], replicated, may hold values from 2 to 10.1
- eta_table: float32 [4], replicated, may hold values from 13 to 18
- gamma_table: float32 [4], replicated, may hold values from 0.4 to 0.8
Outputs:
- charges: float32 [131072], P(('row', 'col'))
Inputs may be any that keep to these rules, and one draw needn't show every extreme that they name: The cells of the blocks are a permutation of all 16 x 16 x 4 cells: each cell holds exactly one block. The mask marks a pair of blocks exactly when their cells are equal or adjacent on the periodic grid in every dimension; it is symmetric and each block is marked with exactly 27 blocks, itself included. `types`: types 2 and 3 grow more common along the atoms, from none in the first 256 atoms to nearly all in the last.
All inputs are finite; a program needn't handle non-finite values.
Results may differ from a plain program's by a relative error of at most 0.0003.
Values sent between devices are 32-bit elements; how exact they have to be, the bound alone decides.
A program may use at most 64 MiB of HBM per device.

v0:
```python
import jax
import jax.numpy as jnp
from jax import lax
from jax.sharding import Mesh
from jax.sharding import PartitionSpec as P

BLOCK = 128
GRID_Z = 4
ITERS = 3
ROW_COL = ("row_0", "row_1", "col_0", "col_1")
ROW = ("row_0", "row_1")
COL = ("col_0", "col_1")
coulomb = 14.4
cutoff = 10.0
cell_side = 11.0
pair_group = 64


def copy_for_each(value, axis):
    devices = lax.axis_size(axis)
    return lax.all_to_all(
        jnp.broadcast_to(value[None], (devices, *value.shape)), axis, 0, 0, tiled=True
    )


def over_copies(value, axis):
    return copy_for_each(value, axis).sum(axis=0)


def over_axes(value, axes):
    far, near = axes
    return over_copies(over_copies(value, near), far)


def in_one(arrays, axis):
    line, at, outs = (jnp.concatenate([a.reshape(-1) for a in arrays]), 0, [])
    subtotal = over_axes(line, axis)
    for a in arrays:
        outs.append(subtotal[at : at + a.size].reshape(a.shape))
        at += a.size
    return tuple(outs)


def in_order(blocks, dim):
    blocks = jnp.moveaxis(blocks, 0, dim)
    lengths = blocks.shape
    return blocks.reshape(*lengths[:dim], lengths[dim] * lengths[dim + 1], *lengths[dim + 2 :])


def gathered_copies(value, axis, dim):
    return in_order(copy_for_each(value, axis), dim)


def in_blocks(value, dim, devices):
    before, after = (value.shape[:dim], value.shape[dim + 1 :])
    return jnp.moveaxis(value.reshape(*before, devices, -1, *after), dim, 0)


def sent_and_summed(value, axis, dim):
    devices = lax.axis_size(axis)
    blocks = lax.all_to_all(in_blocks(value, dim, devices), axis, 0, 0, tiled=True)
    return jnp.sum(blocks, axis=0)


def taper(dist):
    xval = dist / cutoff
    poly = 1.0 + xval**4 * (-35.0 + xval * (84.0 + xval * (-70.0 + 20.0 * xval)))
    return jnp.where(xval < 1.0, poly, 0.0)


def coupling(tgt, src, tgt_cell, src_cell, same, grid):
    half = grid[:, None] // 2
    shift = ((src_cell - tgt_cell + half) % grid[:, None] - half).astype(jnp.float32) * cell_side
    radius_sq = jnp.zeros((tgt.shape[1], tgt.shape[2], src.shape[2]), jnp.float32)
    for comp in range(3):
        delta = shift[comp][:, None, None] + src[comp][:, None, :] - tgt[comp][:, :, None]
        radius_sq = radius_sq + delta * delta
    dist = jnp.sqrt(radius_sq)
    paired = tgt[3][:, :, None] * src[3][:, None, :]
    shield = 1.0 / (paired * jnp.sqrt(paired))
    kern = coulomb * taper(dist) / jnp.cbrt(radius_sq * dist + shield)
    width = tgt.shape[2]
    diag = jnp.arange(width)[:, None] == jnp.arange(width)[None, :]
    return jnp.where(same[:, None, None] & diag[None], 0.0, kern)


def pick(kinds, table):
    return jnp.sum(jnp.where(kinds, table[:, None], 0.0), axis=0)


def paired_sums(residual, image):
    return in_one(
        (jnp.sum(residual * residual, axis=1), jnp.sum(residual * image, axis=1)),
        ("row_0", ("row_1", "col_0", "col_1")),
    )


def per_device(offsets, cells, types, mask, chi_table, eta_table, gamma_table):
    n_row = lax.axis_size(ROW)
    n_col = lax.axis_size(COL)
    row_at = lax.axis_index(ROW)
    col_at = lax.axis_index(COL)
    span = types.shape[0]
    bpd = span // BLOCK
    n_tgt = n_row * bpd
    n_src = n_col * bpd
    grid = jnp.array([n_row, n_src // GRID_Z, GRID_Z], jnp.int32)
    kinds = jnp.arange(chi_table.shape[0])[:, None] == types[None, :]
    chi = pick(kinds, chi_table)
    eta = pick(kinds, eta_table)
    gamma = pick(kinds, gamma_table)
    geo = jnp.concatenate([offsets, gamma[None]], axis=0)
    src_geo = gathered_copies(geo, COL, 1).reshape(4, n_src, BLOCK)
    tgt_geo = lax.all_gather(geo, ROW, axis=1, tiled=True).reshape(4, n_tgt, BLOCK)
    tgt_ids = (
        (jnp.arange(n_row, dtype=jnp.int32)[:, None] * n_col + col_at) * bpd
        + jnp.arange(bpd, dtype=jnp.int32)[None, :]
    ).reshape(n_tgt)
    src_ids = row_at * n_src + jnp.arange(n_src, dtype=jnp.int32)
    tgt_cells = jnp.take(cells, tgt_ids, axis=1)
    src_cells = jnp.take(cells, src_ids, axis=1)
    tile = mask.reshape(n_tgt * n_src)
    count = jnp.sum(tile)
    slots = jnp.nonzero(tile, size=n_tgt * n_src + pair_group, fill_value=0)[0].astype(jnp.int32)
    groups = (count + pair_group - 1) // pair_group
    src_range = jnp.arange(n_src, dtype=jnp.int32)

    def block_kernel(step):
        picked = lax.dynamic_slice_in_dim(slots, step * pair_group, pair_group)
        live = step * pair_group + jnp.arange(pair_group) < count
        tgt_blk = picked // n_src
        src_blk = picked % n_src
        kern = coupling(
            tgt_geo[:, tgt_blk],
            src_geo[:, src_blk],
            tgt_cells[:, tgt_blk],
            src_cells[:, src_blk],
            tgt_ids[tgt_blk] == src_ids[src_blk],
            grid,
        )
        return (jnp.where(live[:, None, None], kern, 0.0), tgt_blk, src_blk)

    def apply(direction):
        remote = lax.all_gather(direction, ROW, axis=1, tiled=True).reshape(2, n_tgt, BLOCK)

        def turn(step, acc):
            kern, tgt_blk, src_blk = block_kernel(step)
            contrib = jnp.einsum(
                "gij,kgi->kgj", kern, remote[:, tgt_blk], precision=lax.Precision.HIGHEST
            )
            owners = (src_range[:, None] == src_blk[None, :]).astype(jnp.float32)
            return acc + jnp.einsum("sg,kgj->ksj", owners, contrib, precision=lax.Precision.HIGHEST)

        acc = lax.fori_loop(0, groups, turn, jnp.zeros((2, n_src, BLOCK), jnp.float32))
        summed = sent_and_summed(acc.reshape(2, n_src * BLOCK), COL, 1)
        return summed + eta[None] * direction

    rhs = jnp.stack([-chi, -jnp.ones_like(chi)], axis=0)
    solution = jnp.zeros_like(rhs)
    residual = rhs
    image = apply(residual)
    norm_now, product = paired_sums(residual, image)
    alpha = norm_now / product
    direction = residual
    along = image
    for step in range(ITERS):
        solution = solution + alpha[:, None] * direction
        residual = residual - alpha[:, None] * along
        if step + 1 < ITERS:
            image = apply(residual)
            norm_next, product = paired_sums(residual, image)
            ratio = norm_next / norm_now
            alpha = norm_next / (product - ratio * norm_next / alpha)
            direction = residual + ratio[:, None] * direction
            along = image + ratio[:, None] * along
            norm_now = norm_next
    totals = over_axes(jnp.sum(solution, axis=1), ("row_0", ("row_1", "col_0", "col_1")))
    return solution[0] - totals[0] / totals[1] * solution[1]


def solution(mesh):
    torus = Mesh(mesh.devices.reshape(8, 2, 8, 4), ("row_0", "row_1", "col_0", "col_1"))
    placed = (P(None, ROW_COL), P(), P(ROW_COL), P(None, COL, ROW, None), P(), P(), P())
    return jax.shard_map(
        per_device, mesh=torus, in_specs=placed, out_specs=P(ROW_COL), check_vma=False
    )
```

profile of v0, /device:TPU:1, one launch (start us, length us, event | category | flops | bytes accessed | tf_op | source)
XLA Modules:
  0.0 372.8 jit_solution(4462579200094896409)
XLA Ops:
  2.2 13.7 %all-to-all-start = ((f32[32,4,256]{2,1,0:T(4,128)}), f32[32,4,256]{2,1,0:T(4,128)S(1)}, u32[]{:S(2)}, u32[]{:S(2)}) async-start(f32[32,4,256]{2,1,0:T(4,128)} %broadcast_in_dim.293), calls=%async_computation | async-start | bytes 262144 | tf_op jit(solution)/shard_map/all_to_all | solution.py:21
  20.4 14.7 %scatter_custom_fusion = s32[2112]{0:T(1024)S(1)} fusion(s32[2048]{0:T(1024)S(1)} %bitcast.241, s32[2048]{0:T(1024)S(1)} %broadcast.958, s32[]{:T(128)} %constant.520.clone.1), kind=kCustom, calls=%fused_computation.302 | custom fusion | flops 2048 | bytes 8452 | tf_op jit(solution)/shard_map/scatter-add | solution.py:124
  35.7 18.5 %all_gather.12 = f32[2,4096]{1,0:T(2,128)S(1)} all-gather(f32[2,256]{1,0:T(2,128)S(1)} %stack.2), channel_id=1, replica_groups=mesh['row_0'=8,'row_1'=2,'col_0'=8,'col_1'=4] {'row_0','row_1'}, dimensions={1}, use_global_device_ids=true | all-gather | bytes 34816 | tf_op jit(solution)/shard_map/all_gather | solution.py:144
  54.9 15.1 %all_gather.13 = f32[4,4096]{1,0:T(4,128)S(1)} all-gather(f32[4,256]{1,0:T(4,128)S(1)} %pad_maximum_fusion), channel_id=1, replica_groups=mesh['row_0'=8,'row_1'=2,'col_0'=8,'col_1'=4] {'row_0','row_1'}, dimensions={1}, use_global_device_ids=true | all-gather | bytes 69632 | tf_op jit(solution)/shard_map/all_gather | solution.py:114
  70.1 21.0 %while.48 = (s32[]{:T(128)}, f32[2,64,128]{2,1,0:T(8,128)S(1)}, s32[]{:T(128)}, s32[2112]{0:T(1024)S(1)}, f32[2,32,128]{2,0,1:T(2,128)S(1)}, /*index=5*/s32[]{:T...) while((s32[]{:T(128)}, f32[2,64,128]{2,1,0:T(8,128)S(1)}, ...), condition=%wide.region_11.13_spmd.clone.clone.clone, body=%wide.region_10.12_spmd.sunk.clone.clone.clone.sunk | while | flops 70322144 | bytes 2021583 | solution.py:154
  76.8 14.2 %fusion.249 = f32[2,64,128]{2,0,1:T(2,128)S(1)} fusion(f32[64,128]{1,0:T(8,128)S(1)} %bitcast.216, f32[64,128]{1,0:T(8,128)S(1)} %bitcast.222, f32[64,128]{1,0:T(8,128)S(1)} %bitcast.220, f32[64,128]{1,0:T(8,128)S(1)} %broadcast_add_fusion.19, f32[64,128]{1,0:T(8,128)S(1)} %bitcast.221, f32[64,128]{1,0:T(8,128)S(1)} %broadcast_add_fusion.20, ...), kind=kOutput, calls=%fused_computation.77.clone.1 | convolution fusion | flops 57671680 | bytes 409728 | tf_op jit(solution)/shard_map/while/body/gij,kgi->kgj/dot_general | solution.py:148
  91.3 18.1 %all_to_all.68 = f32[32,2,256]{2,1,0:T(2,128)S(1)} all-to-all(f32[32,2,256]{2,1,0:T(2,128)S(1)} %copy.39), channel_id=1, replica_groups=mesh['row_0'=8,'row_1'=2,'col_0'=8,'col_1'=4] {'col_0','col_1'}, dimensions={0} | all-to-all | bytes 131072 | tf_op jit(solution)/shard_map/all_to_all | solution.py:61
  109.7 14.1 %all_to_all.69 = f32[64,1,4]{2,1,0:T(1,128)S(1)} all-to-all(f32[64,1,4]{2,1,0:T(1,128)S(1)} %broadcast_in_dim.295), channel_id=1, replica_groups=mesh['row_0'=8,'row_1'=2,'col_0'=8,'col_1'=4] {'row_1','col_0','col_1'}, dimensions={0} | all-to-all | bytes 2048 | tf_op jit(solution)/shard_map/all_to_all | solution.py:21
  124.5 24.5 %all-to-all-start.3 = ((f32[8,1,4]{2,1,0:T(1,128)}), f32[8,1,4]{2,1,0:T(1,128)S(1)}, u32[]{:S(2)}, u32[]{:S(2)}) async-start(f32[8,1,4]{2,1,0:T(1,128)} %broadcast_in_dim.296), calls=%async_computation.3 | async-start | bytes 8192 | tf_op jit(solution)/shard_map/all_to_all | solution.py:21
  155.8 16.5 %all_gather.14 = f32[2,4096]{1,0:T(2,128)S(1)} all-gather(f32[2,256]{1,0:T(2,128)S(1)} %multiply_subtract_fusion.1), channel_id=1, replica_groups=mesh['row_0'=8,'row_1'=2,'col_0'=8,'col_1'=4] {'row_0','row_1'}, dimensions={1}, use_global_device_ids=true | all-gather | bytes 34816 | tf_op jit(solution)/shard_map/all_gather | solution.py:144
  172.4 21.0 %while.49 = (s32[]{:T(128)}, f32[2,64,128]{2,1,0:T(8,128)S(1)}, s32[]{:T(128)}, s32[2112]{0:T(1024)S(1)}, f32[2,32,128]{2,0,1:T(2,128)S(1)}, /*index=5*/s32[]{:T...) while((s32[]{:T(128)}, f32[2,64,128]{2,1,0:T(8,128)S(1)}, ...), condition=%wide.region_19.21_spmd.clone.clone.clone, body=%wide.region_18.20_spmd.sunk.clone.clone.clone.sunk | while | flops 70322144 | bytes 2021583 | solution.py:154
  179.0 14.2 %fusion.258 = f32[2,64,128]{2,0,1:T(2,128)S(1)} fusion(f32[64,128]{1,0:T(8,128)S(1)} %bitcast.217, f32[64,128]{1,0:T(8,128)S(1)} %bitcast.226, f32[64,128]{1,0:T(8,128)S(1)} %bitcast.224, f32[64,128]{1,0:T(8,128)S(1)} %broadcast_add_fusion.22, f32[64,128]{1,0:T(8,128)S(1)} %bitcast.225, f32[64,128]{1,0:T(8,128)S(1)} %broadcast_add_fusion.23, ...), kind=kOutput, calls=%fused_computation.161.clone.1 | convolution fusion | flops 57671680 | bytes 409728 | tf_op jit(solution)/shard_map/while/body/gij,kgi->kgj/dot_general | solution.py:148
  193.5 11.8 %all_to_all.70 = f32[32,2,256]{2,1,0:T(2,128)S(1)} all-to-all(f32[32,2,256]{2,1,0:T(2,128)S(1)} %copy.42), channel_id=1, replica_groups=mesh['row_0'=8,'row_1'=2,'col_0'=8,'col_1'=4] {'col_0','col_1'}, dimensions={0} | all-to-all | bytes 131072 | tf_op jit(solution)/shard_map/all_to_all | solution.py:61
  205.7 14.0 %all_to_all.71 = f32[64,1,4]{2,1,0:T(1,128)S(1)} all-to-all(f32[64,1,4]{2,1,0:T(1,128)S(1)} %broadcast_in_dim.297), channel_id=1, replica_groups=mesh['row_0'=8,'row_1'=2,'col_0'=8,'col_1'=4] {'row_1','col_0','col_1'}, dimensions={0} | all-to-all | bytes 2048 | tf_op jit(solution)/shard_map/all_to_all | solution.py:21
  220.3 24.5 %all-to-all-start.6 = ((f32[8,1,4]{2,1,0:T(1,128)}), f32[8,1,4]{2,1,0:T(1,128)S(1)}, u32[]{:S(2)}, u32[]{:S(2)}) async-start(f32[8,1,4]{2,1,0:T(1,128)} %broadcast_in_dim.298), calls=%async_computation.6 | async-start | bytes 8192 | tf_op jit(solution)/shard_map/all_to_all | solution.py:21
  244.8 6.6 %all-to-all-done.6 = f32[8,1,4]{2,1,0:T(1,128)S(1)} async-done(((f32[8,1,4]{2,1,0:T(1,128)}), f32[8,1,4]{2,1,0:T(1,128)S(1)}, u32[]{:S(2)}, u32[]{:S(2)}) %all-to-all-start.6) | async-done | bytes 160 | tf_op jit(solution)/shard_map/all_to_all | solution.py:21
  251.6 16.5 %all_gather.15 = f32[2,4096]{1,0:T(2,128)S(1)} all-gather(f32[2,256]{1,0:T(2,128)S(1)} %multiply_subtract_fusion), channel_id=1, replica_groups=mesh['row_0'=8,'row_1'=2,'col_0'=8,'col_1'=4] {'row_0','row_1'}, dimensions={1}, use_global_device_ids=true | all-gather | bytes 34816 | tf_op jit(solution)/shard_map/all_gather | solution.py:144
  268.1 21.0 %while.50 = (s32[]{:T(128)}, f32[2,64,128]{2,1,0:T(8,128)S(1)}, s32[]{:T(128)}, s32[2112]{0:T(1024)S(1)}, f32[2,32,128]{2,0,1:T(2,128)S(1)}, /*index=5*/s32[]{:T...) while((s32[]{:T(128)}, f32[2,64,128]{2,1,0:T(8,128)S(1)}, ...), condition=%wide.region_26.28_spmd.clone.clone.clone, body=%wide.region_25.27_spmd.sunk.clone.clone.clone.sunk | while | flops 70322144 | bytes 2021583 | solution.py:154
  274.7 14.2 %fusion.267 = f32[2,64,128]{2,0,1:T(2,128)S(1)} fusion(f32[64,128]{1,0:T(8,128)S(1)} %bitcast.218, f32[64,128]{1,0:T(8,128)S(1)} %bitcast.230, f32[64,128]{1,0:T(8,128)S(1)} %bitcast.228, f32[64,128]{1,0:T(8,128)S(1)} %broadcast_add_fusion.25, f32[64,128]{1,0:T(8,128)S(1)} %bitcast.229, f32[64,128]{1,0:T(8,128)S(1)} %broadcast_add_fusion.26, ...), kind=kOutput, calls=%fused_computation.245.clone.1 | convolution fusion | flops 57671680 | bytes 409728 | tf_op jit(solution)/shard_map/while/body/gij,kgi->kgj/dot_general | solution.py:148
  289.2 11.8 %all_to_all.72 = f32[32,2,256]{2,1,0:T(2,128)S(1)} all-to-all(f32[32,2,256]{2,1,0:T(2,128)S(1)} %copy.45), channel_id=1, replica_groups=mesh['row_0'=8,'row_1'=2,'col_0'=8,'col_1'=4] {'col_0','col_1'}, dimensions={0} | all-to-all | bytes 131072 | tf_op jit(solution)/shard_map/all_to_all | solution.py:61
  301.4 14.0 %all_to_all.73 = f32[64,1,4]{2,1,0:T(1,128)S(1)} all-to-all(f32[64,1,4]{2,1,0:T(1,128)S(1)} %broadcast_in_dim.299), channel_id=1, replica_groups=mesh['row_0'=8,'row_1'=2,'col_0'=8,'col_1'=4] {'row_1','col_0','col_1'}, dimensions={0} | all-to-all | bytes 2048 | tf_op jit(solution)/shard_map/all_to_all | solution.py:21
  315.5 30.9 %all_to_all.74 = f32[8,1,4]{2,1,0:T(1,128)S(1)} all-to-all(f32[8,1,4]{2,1,0:T(1,128)S(1)} %broadcast_in_dim.300), channel_id=1, replica_groups=mesh['row_0'=8,'row_1'=2,'col_0'=8,'col_1'=4] {'row_0'}, dimensions={0} | all-to-all | bytes 256 | tf_op jit(solution)/shard_map/all_to_all | solution.py:21
  346.7 14.5 %all_to_all.75 = f32[64,1,2]{2,1,0:T(1,128)S(1)} all-to-all(f32[64,1,2]{2,1,0:T(1,128)S(1)} %broadcast_in_dim.301), channel_id=1, replica_groups=mesh['row_0'=8,'row_1'=2,'col_0'=8,'col_1'=4] {'row_1','col_0','col_1'}, dimensions={0} | all-to-all | bytes 1024 | tf_op jit(solution)/shard_map/all_to_all | solution.py:21
  361.3 8.9 %all_to_all.76 = f32[8,1,2]{2,1,0:T(1,128)S(1)} all-to-all(f32[8,1,2]{2,1,0:T(1,128)S(1)} %broadcast_in_dim.302), channel_id=1, replica_groups=mesh['row_0'=8,'row_1'=2,'col_0'=8,'col_1'=4] {'row_0'}, dimensions={0} | all-to-all | bytes 128 | tf_op jit(solution)/shard_map/all_to_all | solution.py:21
  (160 shorter events, 38.7 us)
Async XLA Ops:
  0.0 18.2 %copy-start.3 = (s32[3,1024]{1,0:T(4,128)S(1)}, s32[3,1024]{1,0:T(4,128)}, u32[]{:S(2)}) copy-start(s32[3,1024]{1,0:T(4,128)} %param.17) | copy-start | bytes 36868
  2.2 67.9 %all-to-all-start = ((f32[32,4,256]{2,1,0:T(4,128)}), f32[32,4,256]{2,1,0:T(4,128)S(1)}, u32[]{:S(2)}, u32[]{:S(2)}) async-start(f32[32,4,256]{2,1,0:T(4,128)} %broadcast_in_dim.293), calls=%async_computation | async-start | bytes 262144 | tf_op jit(solution)/shard_map/all_to_all | solution.py:21
  18.2 51.9 %copy-start = (s32[3]{0:T(128)S(1)}, s32[3]{0:T(128)}, u32[]{:S(2)}) copy-start(s32[3]{0:T(128)} %constant.962) | copy-start | bytes 40
  18.2 51.9 %copy-start.1 = (s32[3]{0:T(128)S(1)}, s32[3]{0:T(128)}, u32[]{:S(2)}) copy-start(s32[3]{0:T(128)} %constant.963) | copy-start | bytes 40
  18.2 51.9 %copy-start.2 = (s32[3]{0:T(128)S(1)}, s32[3]{0:T(128)}, u32[]{:S(2)}) copy-start(s32[3]{0:T(128)} %constant.964) | copy-start | bytes 40
  124.5 31.1 %all-to-all-start.3 = ((f32[8,1,4]{2,1,0:T(1,128)}), f32[8,1,4]{2,1,0:T(1,128)S(1)}, u32[]{:S(2)}, u32[]{:S(2)}) async-start(f32[8,1,4]{2,1,0:T(1,128)} %broadcast_in_dim.296), calls=%async_computation.3 | async-start | bytes 8192 | tf_op jit(solution)/shard_map/all_to_all | solution.py:21
  220.3 31.1 %all-to-all-start.6 = ((f32[8,1,4]{2,1,0:T(1,128)}), f32[8,1,4]{2,1,0:T(1,128)S(1)}, u32[]{:S(2)}, u32[]{:S(2)}) async-start(f32[8,1,4]{2,1,0:T(1,128)} %broadcast_in_dim.298), calls=%async_computation.6 | async-start | bytes 8192 | tf_op jit(solution)/shard_map/all_to_all | solution.py:21
where the time goes:
time: 374 us; the launch traced here: 373 us
  blocking collectives  205 us (55%)
  starting transfers between devices  62.8 us (17%)
  matrix products  43.2 us (12%)
  other arithmetic  25.8 us (7%)
  local copies, waits for them, and re-layouts  20.5 us (5%)
  waiting for transfers between devices  13.1 us (4%)
    all_to_all x6, blocking collectives, copy_for_each(): lax.all_to_all(jnp.broadcast_to(value[None], (devices, *value.shape)), ax...  96.4 us
    all_to_all x3, starting transfers between devices, copy_for_each(): lax.all_to_all(jnp.broadcast_to(value[None], (devices, *value.shape)), ax...  62.8 us
    all_gather x3, blocking collectives, apply(): lax.all_gather(direction, ROW, axis=1, tiled=True).reshape(2, n_tgt, BLOCK)  51.5 us
    dot_general x3, matrix products, turn(): jnp.einsum('gij,kgi->kgj', kern, remote[:, tgt_blk], precision=lax.Precis...  42.6 us
    all_to_all x3, blocking collectives, sent_and_summed(): lax.all_to_all(in_blocks(value, dim, devices), axis, 0, 0, tiled=True)  41.8 us
    all_gather x1, blocking collectives, per_device(): lax.all_gather(geo, ROW, axis=1, tiled=True).reshape(4, n_tgt, BLOCK)  15.1 us
    scatter-add x1, other arithmetic, per_device(): jnp.nonzero(tile, size=n_tgt * n_src + pair_group, fill_value=0)[0]  14.7 us
    all_to_all x3, waiting for transfers between devices, copy_for_each(): lax.all_to_all(jnp.broadcast_to(value[None], (devices, *value.shape)), ax...  13.1 us
  transfers between devices with their start and end apart: 3, of which 2 were waited for; matrix products, arithmetic and copies ran while one was open for 5% of the time, Pallas kernels for 0%

commit v1 on v0

--- a/solution.py
+++ b/solution.py
@@ -141,7 +141,9 @@
         return (jnp.where(live[:, None, None], kern, 0.0), tgt_blk, src_blk)
 
     def apply(direction):
-        remote = lax.all_gather(direction, ROW, axis=1, tiled=True).reshape(2, n_tgt, BLOCK)
+        remote = jnp.concatenate(
+            lax.all_to_all(jnp.stack([direction] * lax.axis_size(ROW)), ROW, 0, 0), axis=1
+        ).reshape(2, n_tgt, BLOCK)
 
         def turn(step, acc):
             kern, tgt_blk, src_blk = block_kernel(step)

time: 374 us -> 355 us (0.949)
  starting transfers between devices: 62.8 us -> 32 us
  blocking collectives: 205 us -> 215 us
    all_to_all x6 -> x8, blocking collectives: 96.4 us -> 155 us  [copy_for_each(): lax.all_to_all(jnp.broadcast_to(value[None], (devices, *value.shape)), ax...]
    all_gather x3 -> x0, blocking collectives: 51.5 us -> none  [apply(): lax.all_gather(direction, ROW, axis=1, tiled=True).reshape(2, n_tgt, BLOCK)]
    all_to_all x3 -> x1, starting transfers between devices: 62.8 us -> 11.4 us  [copy_for_each(): lax.all_to_all(jnp.broadcast_to(value[None], (devices, *value.shape)), ax...]
    all_to_all x0 -> x3, starting transfers between devices: none -> 20.6 us  [apply(): lax.all_to_all(jnp.stack([direction] * lax.axis_size(ROW)), ROW, 0, 0)]
    all_to_all x0 -> x3, waiting for transfers between devices: none -> 15 us  [apply(): lax.all_to_all(jnp.stack([direction] * lax.axis_size(ROW)), ROW, 0, 0)]
    all_to_all x3 -> x1, waiting for transfers between devices: 13.1 us -> 0.01 us  [copy_for_each(): lax.all_to_all(jnp.broadcast_to(value[None], (devices, *value.shape)), ax...]
  transfers between devices with their start and end apart: 3 -> 4, of which waited for: 2 -> 2; matrix products, arithmetic and copies ran while one was open for 5% -> 6% of each run, Pallas kernels for 0% -> 0%
where the time goes in v1:
time: 355 us; the launch traced here: 354 us
  blocking collectives  215 us (61%)
  matrix products  43.2 us (12%)
  starting transfers between devices  32 us (9%)
  other arithmetic  25.1 us (7%)
  local copies, waits for them, and re-layouts  21.8 us (6%)
  waiting for transfers between devices  15 us (4%)
    all_to_all x8, blocking collectives, copy_for_each(): lax.all_to_all(jnp.broadcast_to(value[None], (devices, *value.shape)), ax...  155 us
    dot_general x3, matrix products, turn(): jnp.einsum('gij,kgi->kgj', kern, remote[:, tgt_blk], precision=lax.Precis...  42.6 us
    all_to_all x3, blocking collectives, sent_and_summed(): lax.all_to_all(in_blocks(value, dim, devices), axis, 0, 0, tiled=True)  41.8 us
    all_to_all x3, starting transfers between devices, apply(): lax.all_to_all(jnp.stack([direction] * lax.axis_size(ROW)), ROW, 0, 0)  20.6 us
    all_gather x1, blocking collectives, per_device(): lax.all_gather(geo, ROW, axis=1, tiled=True).reshape(4, n_tgt, BLOCK)  17.6 us
    all_to_all x3, waiting for transfers between devices, apply(): lax.all_to_all(jnp.stack([direction] * lax.axis_size(ROW)), ROW, 0, 0)  15 us
    scatter-add x1, other arithmetic, per_device(): jnp.nonzero(tile, size=n_tgt * n_src + pair_group, fill_value=0)[0]  14.7 us
    all_to_all x1, starting transfers between devices, copy_for_each(): lax.all_to_all(jnp.broadcast_to(value[None], (devices, *value.shape)), ax...  11.4 us
  transfers between devices with their start and end apart: 4, of which 2 were waited for; matrix products, arithmetic and copies ran while one was open for 6% of the time, Pallas kernels for 0%

profile of v1, /device:TPU:1, one launch (start us, length us, event | category | flops | bytes accessed | tf_op | source)
XLA Modules:
  0.0 354.4 jit_solution(1485966386819533454)
XLA Ops:
  1.4 10.1 %all-to-all-start = ((f32[16,2,256]{2,1,0:T(2,128)}), f32[16,2,256]{2,1,0:T(2,128)S(1)}, u32[]{:S(2)}, u32[]{:S(2)}) async-start(f32[16,2,256]{2,1,0:T(2,128)} %stack.9), calls=%async_computation | async-start | bytes 65536 | tf_op jit(solution)/shard_map/all_to_all | solution.py:145
  16.8 14.7 %scatter_custom_fusion = s32[2112]{0:T(1024)S(1)} fusion(s32[2048]{0:T(1024)S(1)} %bitcast.247, s32[2048]{0:T(1024)S(1)} %broadcast.964, s32[]{:T(128)} %constant.520.clone.1), kind=kCustom, calls=%fused_computation.302 | custom fusion | flops 2048 | bytes 8452 | tf_op jit(solution)/shard_map/scatter-add | solution.py:124
  33.5 11.4 %all-to-all-start.1 = ((f32[32,4,256]{2,1,0:T(4,128)}), f32[32,4,256]{2,1,0:T(4,128)S(1)}, u32[]{:S(2)}, u32[]{:S(2)}) async-start(f32[32,4,256]{2,1,0:T(4,128)} %broadcast_in_dim.293), calls=%async_computation.1 | async-start | bytes 262144 | tf_op jit(solution)/shard_map/all_to_all | solution.py:21
  44.9 17.6 %all_gather.3 = f32[4,4096]{1,0:T(4,128)S(1)} all-gather(f32[4,256]{1,0:T(4,128)S(1)} %pad_maximum_fusion), channel_id=1, replica_groups=mesh['row_0'=8,'row_1'=2,'col_0'=8,'col_1'=4] {'row_0','row_1'}, dimensions={1}, use_global_device_ids=true | all-gather | bytes 69632 | tf_op jit(solution)/shard_map/all_gather | solution.py:114
  62.7 21.0 %while.48 = (s32[]{:T(128)}, f32[2,64,128]{2,1,0:T(8,128)S(1)}, s32[]{:T(128)}, s32[2112]{0:T(1024)S(1)}, f32[2,32,128]{2,0,1:T(2,128)S(1)}, /*index=5*/s32[]{:T...) while((s32[]{:T(128)}, f32[2,64,128]{2,1,0:T(8,128)S(1)}, ...), condition=%wide.region_11.13_spmd.clone.clone.clone, body=%wide.region_10.12_spmd.sunk.clone.clone.clone.sunk | while | flops 70322144 | bytes 2021583 | solution.py:156
  69.3 14.2 %fusion.249 = f32[2,64,128]{2,0,1:T(2,128)S(1)} fusion(f32[64,128]{1,0:T(8,128)S(1)} %bitcast.222, f32[64,128]{1,0:T(8,128)S(1)} %bitcast.228, f32[64,128]{1,0:T(8,128)S(1)} %bitcast.226, f32[64,128]{1,0:T(8,128)S(1)} %broadcast_add_fusion.19, f32[64,128]{1,0:T(8,128)S(1)} %bitcast.227, f32[64,128]{1,0:T(8,128)S(1)} %broadcast_add_fusion.20, ...), kind=kOutput, calls=%fused_computation.77.clone.1 | convolution fusion | flops 57671680 | bytes 409728 | tf_op jit(solution)/shard_map/while/body/gij,kgi->kgj/dot_general | solution.py:150
  83.8 18.1 %all_to_all.83 = f32[32,2,256]{2,1,0:T(2,128)S(1)} all-to-all(f32[32,2,256]{2,1,0:T(2,128)S(1)} %copy.39), channel_id=1, replica_groups=mesh['row_0'=8,'row_1'=2,'col_0'=8,'col_1'=4] {'col_0','col_1'}, dimensions={0} | all-to-all | bytes 131072 | tf_op jit(solution)/shard_map/all_to_all | solution.py:61
  102.3 14.1 %all_to_all.84 = f32[64,1,4]{2,1,0:T(1,128)S(1)} all-to-all(f32[64,1,4]{2,1,0:T(1,128)S(1)} %broadcast_in_dim.295), channel_id=1, replica_groups=mesh['row_0'=8,'row_1'=2,'col_0'=8,'col_1'=4] {'row_1','col_0','col_1'}, dimensions={0} | all-to-all | bytes 2048 | tf_op jit(solution)/shard_map/all_to_all | solution.py:21
  116.5 31.4 %all_to_all.85 = f32[8,1,4]{2,1,0:T(1,128)S(1)} all-to-all(f32[8,1,4]{2,1,0:T(1,128)S(1)} %broadcast_in_dim.296), channel_id=1, replica_groups=mesh['row_0'=8,'row_1'=2,'col_0'=8,'col_1'=4] {'row_0'}, dimensions={0} | all-to-all | bytes 256 | tf_op jit(solution)/shard_map/all_to_all | solution.py:21
  148.7 5.2 %all-to-all-start.5 = ((f32[16,2,256]{2,1,0:T(2,128)}), f32[16,2,256]{2,1,0:T(2,128)S(1)}, u32[]{:S(2)}, u32[]{:S(2)}) async-start(f32[16,2,256]{2,1,0:T(2,128)} %stack.10), calls=%async_computation.5 | async-start | bytes 65536 | tf_op jit(solution)/shard_map/all_to_all | solution.py:145
  153.9 7.5 %all-to-all-done.5 = f32[16,2,256]{2,1,0:T(2,128)S(1)} async-done(((f32[16,2,256]{2,1,0:T(2,128)}), f32[16,2,256]{2,1,0:T(2,128)S(1)}, u32[]{:S(2)}, u32[]{:S(2)}) %all-to-all-start.5) | async-done | bytes 32800 | tf_op jit(solution)/shard_map/all_to_all | solution.py:145
  161.4 21.0 %while.49 = (s32[]{:T(128)}, f32[2,64,128]{2,1,0:T(8,128)S(1)}, s32[]{:T(128)}, s32[2112]{0:T(1024)S(1)}, f32[2,32,128]{2,0,1:T(2,128)S(1)}, /*index=5*/s32[]{:T...) while((s32[]{:T(128)}, f32[2,64,128]{2,1,0:T(8,128)S(1)}, ...), condition=%wide.region_19.21_spmd.clone.clone.clone, body=%wide.region_18.20_spmd.sunk.clone.clone.clone.sunk | while | flops 70322144 | bytes 2021583 | solution.py:156
  168.0 14.2 %fusion.258 = f32[2,64,128]{2,0,1:T(2,128)S(1)} fusion(f32[64,128]{1,0:T(8,128)S(1)} %bitcast.223, f32[64,128]{1,0:T(8,128)S(1)} %bitcast.232, f32[64,128]{1,0:T(8,128)S(1)} %bitcast.230, f32[64,128]{1,0:T(8,128)S(1)} %broadcast_add_fusion.22, f32[64,128]{1,0:T(8,128)S(1)} %bitcast.231, f32[64,128]{1,0:T(8,128)S(1)} %broadcast_add_fusion.23, ...), kind=kOutput, calls=%fused_computation.161.clone.1 | convolution fusion | flops 57671680 | bytes 409728 | tf_op jit(solution)/shard_map/while/body/gij,kgi->kgj/dot_general | solution.py:150
  182.5 11.8 %all_to_all.86 = f32[32,2,256]{2,1,0:T(2,128)S(1)} all-to-all(f32[32,2,256]{2,1,0:T(2,128)S(1)} %copy.42), channel_id=1, replica_groups=mesh['row_0'=8,'row_1'=2,'col_0'=8,'col_1'=4] {'col_0','col_1'}, dimensions={0} | all-to-all | bytes 131072 | tf_op jit(solution)/shard_map/all_to_all | solution.py:61
  194.7 14.0 %all_to_all.87 = f32[64,1,4]{2,1,0:T(1,128)S(1)} all-to-all(f32[64,1,4]{2,1,0:T(1,128)S(1)} %broadcast_in_dim.297), channel_id=1, replica_groups=mesh['row_0'=8,'row_1'=2,'col_0'=8,'col_1'=4] {'row_1','col_0','col_1'}, dimensions={0} | all-to-all | bytes 2048 | tf_op jit(solution)/shard_map/all_to_all | solution.py:21
  208.8 29.1 %all_to_all.88 = f32[8,1,4]{2,1,0:T(1,128)S(1)} all-to-all(f32[8,1,4]{2,1,0:T(1,128)S(1)} %broadcast_in_dim.298), channel_id=1, replica_groups=mesh['row_0'=8,'row_1'=2,'col_0'=8,'col_1'=4] {'row_0'}, dimensions={0} | all-to-all | bytes 256 | tf_op jit(solution)/shard_map/all_to_all | solution.py:21
  244.0 7.5 %all-to-all-done.9 = f32[16,2,256]{2,1,0:T(2,128)S(1)} async-done(((f32[16,2,256]{2,1,0:T(2,128)}), f32[16,2,256]{2,1,0:T(2,128)S(1)}, u32[]{:S(2)}, u32[]{:S(2)}) %all-to-all-start.9) | async-done | bytes 32800 | tf_op jit(solution)/shard_map/all_to_all | solution.py:145
  251.5 21.0 %while.50 = (s32[]{:T(128)}, f32[2,64,128]{2,1,0:T(8,128)S(1)}, s32[]{:T(128)}, s32[2112]{0:T(1024)S(1)}, f32[2,32,128]{2,0,1:T(2,128)S(1)}, /*index=5*/s32[]{:T...) while((s32[]{:T(128)}, f32[2,64,128]{2,1,0:T(8,128)S(1)}, ...), condition=%wide.region_26.28_spmd.clone.clone.clone, body=%wide.region_25.27_spmd.sunk.clone.clone.clone.sunk | while | flops 70322144 | bytes 2021583 | solution.py:156
  258.1 14.2 %fusion.267 = f32[2,64,128]{2,0,1:T(2,128)S(1)} fusion(f32[64,128]{1,0:T(8,128)S(1)} %bitcast.224, f32[64,128]{1,0:T(8,128)S(1)} %bitcast.236, f32[64,128]{1,0:T(8,128)S(1)} %bitcast.234, f32[64,128]{1,0:T(8,128)S(1)} %broadcast_add_fusion.25, f32[64,128]{1,0:T(8,128)S(1)} %bitcast.235, f32[64,128]{1,0:T(8,128)S(1)} %broadcast_add_fusion.26, ...), kind=kOutput, calls=%fused_computation.245.clone.1 | convolution fusion | flops 57671680 | bytes 409728 | tf_op jit(solution)/shard_map/while/body/gij,kgi->kgj/dot_general | solution.py:150
  272.6 11.8 %all_to_all.89 = f32[32,2,256]{2,1,0:T(2,128)S(1)} all-to-all(f32[32,2,256]{2,1,0:T(2,128)S(1)} %copy.45), channel_id=1, replica_groups=mesh['row_0'=8,'row_1'=2,'col_0'=8,'col_1'=4] {'col_0','col_1'}, dimensions={0} | all-to-all | bytes 131072 | tf_op jit(solution)/shard_map/all_to_all | solution.py:61
  284.7 14.0 %all_to_all.90 = f32[64,1,4]{2,1,0:T(1,128)S(1)} all-to-all(f32[64,1,4]{2,1,0:T(1,128)S(1)} %broadcast_in_dim.299), channel_id=1, replica_groups=mesh['row_0'=8,'row_1'=2,'col_0'=8,'col_1'=4] {'row_1','col_0','col_1'}, dimensions={0} | all-to-all | bytes 2048 | tf_op jit(solution)/shard_map/all_to_all | solution.py:21
  298.9 29.1 %all_to_all.91 = f32[8,1,4]{2,1,0:T(1,128)S(1)} all-to-all(f32[8,1,4]{2,1,0:T(1,128)S(1)} %broadcast_in_dim.300), channel_id=1, replica_groups=mesh['row_0'=8,'row_1'=2,'col_0'=8,'col_1'=4] {'row_0'}, dimensions={0} | all-to-all | bytes 256 | tf_op jit(solution)/shard_map/all_to_all | solution.py:21
  328.3 14.5 %all_to_all.92 = f32[64,1,2]{2,1,0:T(1,128)S(1)} all-to-all(f32[64,1,2]{2,1,0:T(1,128)S(1)} %broadcast_in_dim.301), channel_id=1, replica_groups=mesh['row_0'=8,'row_1'=2,'col_0'=8,'col_1'=4] {'row_1','col_0','col_1'}, dimensions={0} | all-to-all | bytes 1024 | tf_op jit(solution)/shard_map/all_to_all | solution.py:21
  342.9 8.9 %all_to_all.93 = f32[8,1,2]{2,1,0:T(1,128)S(1)} all-to-all(f32[8,1,2]{2,1,0:T(1,128)S(1)} %broadcast_in_dim.302), channel_id=1, replica_groups=mesh['row_0'=8,'row_1'=2,'col_0'=8,'col_1'=4] {'row_0'}, dimensions={0} | all-to-all | bytes 128 | tf_op jit(solution)/shard_map/all_to_all | solution.py:21
  (164 shorter events, 38.1 us)
Async XLA Ops:
  1.4 31.4 %all-to-all-start = ((f32[16,2,256]{2,1,0:T(2,128)}), f32[16,2,256]{2,1,0:T(2,128)S(1)}, u32[]{:S(2)}, u32[]{:S(2)}) async-start(f32[16,2,256]{2,1,0:T(2,128)} %stack.9), calls=%async_computation | async-start | bytes 65536 | tf_op jit(solution)/shard_map/all_to_all | solution.py:145
  13.0 19.9 %copy-start.3 = (f32[3,256]{1,0:T(4,128)S(1)}, f32[3,256]{1,0:T(4,128)}, u32[]{:S(2)}) copy-start(f32[3,256]{1,0:T(4,128)} %param.16) | copy-start | bytes 9220
  14.8 47.8 %copy-start = (s32[3]{0:T(128)S(1)}, s32[3]{0:T(128)}, u32[]{:S(2)}) copy-start(s32[3]{0:T(128)} %constant.962) | copy-start | bytes 40
  14.8 47.8 %copy-start.1 = (s32[3]{0:T(128)S(1)}, s32[3]{0:T(128)}, u32[]{:S(2)}) copy-start(s32[3]{0:T(128)} %constant.963) | copy-start | bytes 40
  14.8 47.8 %copy-start.2 = (s32[3]{0:T(128)S(1)}, s32[3]{0:T(128)}, u32[]{:S(2)}) copy-start(s32[3]{0:T(128)} %constant.964) | copy-start | bytes 40
  33.5 29.1 %all-to-all-start.1 = ((f32[32,4,256]{2,1,0:T(4,128)}), f32[32,4,256]{2,1,0:T(4,128)S(1)}, u32[]{:S(2)}, u32[]{:S(2)}) async-start(f32[32,4,256]{2,1,0:T(4,128)} %broadcast_in_dim.293), calls=%async_computation.1 | async-start | bytes 262144 | tf_op jit(solution)/shard_map/all_to_all | solution.py:21
  148.7 12.7 %all-to-all-start.5 = ((f32[16,2,256]{2,1,0:T(2,128)}), f32[16,2,256]{2,1,0:T(2,128)S(1)}, u32[]{:S(2)}, u32[]{:S(2)}) async-start(f32[16,2,256]{2,1,0:T(2,128)} %stack.10), calls=%async_computation.5 | async-start | bytes 65536 | tf_op jit(solution)/shard_map/all_to_all | solution.py:145
  238.7 12.7 %all-to-all-start.9 = ((f32[16,2,256]{2,1,0:T(2,128)}), f32[16,2,256]{2,1,0:T(2,128)S(1)}, u32[]{:S(2)}, u32[]{:S(2)}) async-start(f32[16,2,256]{2,1,0:T(2,128)} %stack.11), calls=%async_computation.9 | async-start | bytes 65536 | tf_op jit(solution)/shard_map/all_to_all | solution.py:145
